TPU v7x, 32 devices: a whole 2x2x4 slice. The times are simulated.
32 devices in a mesh: groups: 2 (over y), pts: 4 (over z), cb: 4 (over x, core).
Axes of the slice: x: 2, y: 2, z: 4, core: 2. Of those that a mesh axis runs over, the one named last changes fastest.
Arguments:
- points: bfloat16 [16384, 768], P(('groups', 'pts')), parts along dimension 0, may hold values from -60 to 60
- code_one: int32 [16384], P(('groups', 'pts')), parts along dimension 0, may hold values from 0 to 2047
- code_two: int32 [16384], P(('groups', 'pts')), parts along dimension 0, may hold values from 0 to 2047
- cent_one: bfloat16 [4096, 768], P(('groups', 'cb')), parts along dimension 0, may hold values from -6 to 6
- cent_two: bfloat16 [4096, 768], P(('groups', 'cb')), parts along dimension 0, may hold values from -6 to 6
Outputs:
- new_one: bfloat16 [4096, 768], P(('groups', 'cb')), parts along dimension 0
- new_two: bfloat16 [4096, 768], P(('groups', 'cb')), parts along dimension 0
- distortion: float32 [4], P('groups'), parts along dimension 0
There are 2 independent parts, one for each index of `groups`. A program takes and returns all parts, laid end to end along the dimension named above; each array names one. Nothing has to cross between parts.
All inputs are finite; a program needn't handle non-finite values.
Results may differ from a plain program's by a relative error of at most 0.0014.
Values may be sent and summed in bfloat16 or wider, within the bound.
A program may use at most 64 MiB of HBM per device.

v0:
```python
import jax
import jax.numpy as jnp
from jax import lax
from jax.sharding import PartitionSpec as P


def nearest_local(data, cents):
    sq = jnp.sum(jnp.square(data.astype(jnp.float32)), axis=1)
    csq = jnp.sum(jnp.square(cents.astype(jnp.float32)), axis=1)
    cross = lax.dot_general(
        data, cents, (((1,), (1,)), ((), ())), preferred_element_type=jnp.float32
    )
    dist = sq[:, None] - 2.0 * cross + csq[None, :]
    local_min = jnp.min(dist, axis=1)
    best = lax.pmin(local_min, "cb")
    return jnp.sum(best)


def section_update(data, codes, cents):
    rows = cents.shape[0]
    first = lax.axis_index("cb") * rows
    labels = first + lax.broadcasted_iota(jnp.int32, (1, rows), 1)
    onehot = (codes[:, None] == labels).astype(jnp.bfloat16)
    sums = lax.dot_general(
        onehot, data, (((0,), (0,)), ((), ())), preferred_element_type=jnp.float32
    )
    counts = jnp.sum(onehot.astype(jnp.float32), axis=0)
    share_sums, share_counts = (
        lax.psum_scatter(sums, "pts", scatter_dimension=0, tiled=True),
        lax.psum_scatter(counts, "pts", scatter_dimension=0, tiled=True),
    )
    share_rows = share_sums.shape[0]
    old_rows = lax.dynamic_slice_in_dim(cents, lax.axis_index("pts") * share_rows, share_rows, 0)
    return ((share_sums + old_rows.astype(jnp.float32)) / (share_counts + 1.0)[:, None]).astype(
        jnp.bfloat16
    )


def section_total(value):
    return lax.psum(value, "pts")


def local(points, code_one, code_two, cent_one, cent_two):
    rows = cent_one.shape[0]
    width = points.shape[1]
    npts = lax.axis_size("pts")
    ncb = lax.axis_size("cb")
    first = lax.axis_index("cb") * rows
    first_local = nearest_local(points, cent_one)
    updated_one = section_update(points, code_one, cent_one)
    gathered = lax.all_gather(updated_one, ("pts", "cb"), axis=0, tiled=True)
    share_rows = updated_one.shape[0]
    codebook = jnp.swapaxes(gathered.reshape(npts, ncb, share_rows, width), 0, 1).reshape(
        rows * ncb, width
    )
    new_one = lax.dynamic_slice_in_dim(codebook, first, rows, 0)
    looked = jnp.take(codebook, code_one, axis=0)
    residual = (points.astype(jnp.float32) - looked.astype(jnp.float32)).astype(jnp.bfloat16)
    updated_two = section_update(residual, code_two, cent_two)
    new_two = lax.all_gather(updated_two, "pts", axis=0, tiled=True)
    second_local = nearest_local(residual, cent_two)
    first_sum = section_total(first_local)
    second_sum = section_total(second_local)
    scale = jnp.float32(points.shape[0] * npts * width)
    distortion = jnp.stack([first_sum, second_sum]) / scale
    return (new_one, new_two, distortion)


def solution(mesh):
    return jax.shard_map(
        local,
        mesh=mesh,
        in_specs=(
            P(("groups", "pts"), None),
            P(("groups", "pts")),
            P(("groups", "pts")),
            P(("groups", "cb"), None),
            P(("groups", "cb"), None),
        ),
        out_specs=(P(("groups", "cb"), None), P(("groups", "cb"), None), P("groups")),
        check_vma=False,
    )
```

profile of v0, /device:TPU:0, one launch (start us, length us, event | category | flops | bytes accessed | tf_op | source)
XLA Modules:
  0.0 180.3 jit_solution(905735486691300784)
XLA Ops:
  7.3 5.2 %fusion.4 = f32[512,768]{1,0:T(8,128)} fusion(bf16[2048,768]{1,0:T(8,128)(2,1)} %param.5, s32[512]{0:T(512)S(1)} %iota_add_fusion, s32[2048]{0:T(1024)} %param.6), kind=kOutput, calls=%fused_computation.10 | convolution fusion | flops 1611661312 | bytes 4728832 | tf_op jit(solution)/shard_map/dot_general | solution.py:24
  13.8 1.2 convert_reduce_fusion
  15.1 13.9 %all-reduce = f32[512]{0:T(512)S(1)} all-reduce(f32[512]{0:T(512)S(1)} %get-tuple-element.4), channel_id=3, replica_groups=mesh['groups'=2,'pts'=4,'cb'=4] {'pts'}, use_global_device_ids=true, to_apply=%region_2.0.clone | all-reduce | flops 512 | bytes 4096
  29.0 21.9 %reduce-scatter.3.cloned.1.call-done = f32[128,768]{1,0:T(8,128)} async-done(((f32[512,768]{1,0:T(8,128)}), f32[128,768]{1,0:T(8,128)}) %reduce-scatter.3.cloned.1.call-update) | async-done | bytes 393232 | tf_op jit(solution)/shard_map/reduce_scatter | solution.py:29
  50.9 1.8 %divide_convert_fusion.1 = bf16[128,768]{1,0:T(8,128)(2,1)} fusion(f32[128,768]{1,0:T(8,128)} %reduce-scatter.3.cloned.1.call-done, f32[128]{0:T(128)S(1)} %dynamic-slice_add_fusion.1, bf16[512,768]{1,0:T(8,128)(2,1)} %param.8, s32[]{:T(128)S(6)} %select_n.16), kind=kLoop, calls=%fused_computation.23 | loop fusion | flops 393216 | bytes 786948 | tf_op jit(solution)/shard_map/convert_element_type | solution.py:34
  52.8 45.4 %all-gather.2.cloned.1.call-done = bf16[2048,768]{1,0:T(8,128)(2,1)} async-done(((bf16[128,768]{1,0:T(8,128)(2,1)}), bf16[2048,768]{1,0:T(8,128)(2,1)}) %all-gather.2.cloned.1.call-update) | async-done | bytes 3145744 | tf_op jit(solution)/shard_map/all_gather | solution.py:51
  98.2 2.1 %copy.10 = bf16[4,4,128,768]{3,2,1,0:T(8,128)(2,1)S(1)} copy(bf16[4,4,128,768]{3,2,0,1:T(8,128)(2,1)} %bitcast.15) | data formatting | bytes 6291456 | tf_op jit(solution)/shard_map/transpose | solution.py:53
  100.3 9.4 %gather_fusion = bf16[2048,768]{1,0:T(8,128)(2,1)} fusion(bf16[2048,768]{1,0:T(8,128)(2,1)S(1)} %bitcast.13, s32[2048]{0:T(1024)S(1)} %fusion.10), kind=kCustom, calls=%fused_computation | custom fusion | bytes 6299648 | tf_op jit(solution)/shard_map/jit(_take)/gather | solution.py:57
  109.7 4.3 %multiply_reduce_fusion = (f32[2048]{0:T(1024)S(1)}, bf16[2048,768]{1,0:T(8,128)(2,1)S(1)}, f32[2048]{0:T(1024)S(1)}) fusion(bf16[2048,768]{1,0:T(8,128)(2,1)} %gather_fusion, pred[2048]{0:T(1024)(128)(4,1)S(1)} %compare_and_fusion, bf16[2048,768]{1,0:T(8,128)(2,1)} %param.5), kind=kLoop, calls=%fused_computation.5 | loop fusion | flops 15724544 | bytes 9455616 | tf_op jit(solution)/shard_map/reduce_sum | solution.py:8
  114.0 1.7 copy-done.1
  115.7 3.3 %fusion.2 = f32[512,768]{1,0:T(8,128)} fusion(bf16[2048,768]{1,0:T(8,128)(2,1)S(1)} %get-tuple-element.11, s32[512]{0:T(512)S(1)} %iota_add_fusion, s32[2048]{0:T(1024)S(1)} %copy-done.4), kind=kOutput, calls=%fused_computation.7 | convolution fusion | flops 1611661312 | bytes 4728832 | tf_op jit(solution)/shard_map/dot_general | solution.py:24
  119.0 1.4 multiply_reduce_fusion.2
  120.4 1.4 multiply_reduce_fusion.1
  121.8 4.3 %add_reduce_fusion = f32[2048]{0:T(1024)S(1)} fusion(bf16[2048,768]{1,0:T(8,128)(2,1)} %copy-done.1, bf16[512,768]{1,0:T(8,128)(2,1)} %param.9, f32[512]{0:T(512)S(1)} %multiply_reduce_fusion.1, f32[2048]{0:T(1024)S(1)} %get-tuple-element.10), kind=kOutput, calls=%fused_computation.12 | convolution fusion | flops 1614804992 | bytes 3950592 | tf_op jit(solution)/shard_map/dot_general | solution.py:10
  126.2 1.8 %add_reduce_fusion.1 = f32[2048]{0:T(1024)S(1)} fusion(bf16[2048,768]{1,0:T(8,128)(2,1)S(1)} %copy-done, bf16[512,768]{1,0:T(8,128)(2,1)S(1)} %copy-done.2, f32[512]{0:T(512)S(1)} %multiply_reduce_fusion.2, f32[2048]{0:T(1024)S(1)} %get-tuple-element.12), kind=kOutput, calls=%fused_computation.13 | convolution fusion | flops 1614804992 | bytes 3950592 | tf_op jit(solution)/shard_map/dot_general | solution.py:10
  128.0 11.0 %all-reduce.3 = (f32[2048]{0:T(1024)S(1)}, f32[2048]{0:T(1024)S(1)}) all-reduce(f32[2048]{0:T(1024)S(1)} %add_reduce_fusion, f32[2048]{0:T(1024)S(1)} %add_reduce_fusion.1), channel_id=1, replica_groups=mesh['groups'=2,'pts'=4,'cb'=4] {'cb'}, use_global_device_ids=true, to_apply=%region_15.16 | all-reduce | flops 4096 | bytes 32768 | tf_op jit(solution)/shard_map/pmin | solution.py:15
  139.0 0.6 reduce_sum.79
  139.6 0.6 reduce_sum.76
  140.2 11.1 %all-reduce.2 = (f32[512]{0:T(512)S(1)}, f32[1]{0:T(128)}, f32[1]{0:T(128)}) all-reduce(f32[512]{0:T(512)S(1)} %get-tuple-element.3, f32[1]{0:T(128)} %bitcast.4, f32[1]{0:T(128)} %bitcast.3), channel_id=5, replica_groups=mesh['groups'=2,'pts'=4,'cb'=4] {'pts'}, use_global_device_ids=true, to_apply=%region_5.0.clone | all-reduce | flops 514 | bytes 4112
  151.4 1.9 %maximum_multiply_fusion = f32[2]{0:T(128)} fusion(f32[1]{0:T(128)} %get-tuple-element.6, f32[1]{0:T(128)} %get-tuple-element.7), kind=kLoop, calls=%fused_computation.29 | loop fusion | flops 4 | bytes 16 | tf_op jit(solution)/shard_map/div | solution.py:65
  153.2 0.9 constant_dynamic-slice_fusion
  154.2 1.1 divide_convert_fusion
  155.3 17.6 %all_gather.7 = bf16[512,768]{1,0:T(8,128)(2,1)S(1)} all-gather(bf16[128,768]{1,0:T(8,128)(2,1)S(1)} %divide_convert_fusion), channel_id=1, replica_groups=mesh['groups'=2,'pts'=4,'cb'=4] {'pts'}, dimensions={0}, use_global_device_ids=true | all-gather | bytes 983040 | tf_op jit(solution)/shard_map/all_gather | solution.py:60
  172.9 0.9 copy.12
  (24 shorter events, 1.0 us)
Async XLA Ops:
  7.2 43.7 %reduce-scatter.3.cloned.1.call-start = ((), (), s32[]{:S(2)}) async-start(), calls=%async_computation.2 | async-start | bytes 1966080 | tf_op jit(solution)/shard_map/reduce_scatter | solution.py:29
  7.2 5.3 %copy-start.5 = (u32[32]{0:T(128)S(1)}, u32[32]{0:T(128)}, u32[]{:S(2)}) copy-start(u32[32]{0:T(128)} %constant.42) | copy-start | bytes 388
  7.2 6.6 %copy-start.3 = (s32[2048]{0:T(1024)S(1)}, s32[2048]{0:T(1024)}, u32[]{:S(2)}) copy-start(s32[2048]{0:T(1024)} %param.6) | copy-start | bytes 24580
  7.3 6.6 %copy-start.4 = (s32[2048]{0:T(1024)S(1)}, s32[2048]{0:T(1024)}, u32[]{:S(2)}) copy-start(s32[2048]{0:T(1024)} %param.7) | copy-start | bytes 24580
  12.5 85.7 %all-gather.2.cloned.1.call-start = ((), (), s32[]{:S(2)}) async-start(), calls=%async_computation.3 | async-start | bytes 3342336 | tf_op jit(solution)/shard_map/all_gather | solution.py:51
  52.8 101.4 %reduce-scatter.5.cloned.1.call-start = ((), (), s32[]{:S(2)}) async-start(), calls=%async_computation.4 | async-start | bytes 1966080 | tf_op jit(solution)/shard_map/reduce_scatter | solution.py:29
  114.0 1.7 copy-start.1
  121.8 4.4 %copy-start = (bf16[2048,768]{1,0:T(8,128)(2,1)S(1)}, bf16[2048,768]{1,0:T(8,128)(2,1)}, u32[]{:S(2)}) copy-start(bf16[2048,768]{1,0:T(8,128)(2,1)} %param.5) | copy-start | bytes 9437188
  121.8 4.4 %copy-start.2 = (bf16[512,768]{1,0:T(8,128)(2,1)S(1)}, bf16[512,768]{1,0:T(8,128)(2,1)}, u32[]{:S(2)}) copy-start(bf16[512,768]{1,0:T(8,128)(2,1)} %param.8) | copy-start | bytes 2359300
Sparse Core Ops, SparseCore 0:
  12.6 38.2 reduce-scatter.2
  53.8 44.3 all-gather.1
  119.2 34.0 reduce-scatter.4
where the time goes:
time: 181 us; the launch traced here: 180 us
  waiting for transfers between devices  67.3 us (37%)
  blocking collectives  53.6 us (30%)
  local copies, waits for them, and re-layouts  15.6 us (9%)
  matrix products  14.7 us (8%)
  between operations  14.6 us (8%)
  other arithmetic  14.5 us (8%)
    all_gather x1, waiting for transfers between devices, local(): gathered = lax.all_gather(updated_one, ('pts', 'cb'), axis=0, tiled=True)  45.4 us
    unnamed x2, blocking collectives  25 us
    reduce_scatter x2, waiting for transfers between devices, section_update(): lax.psum_scatter(sums, 'pts', scatter_dimension=0, tiled=True)  21.9 us
    all_gather x1, blocking collectives, local(): new_two = lax.all_gather(updated_two, 'pts', axis=0, tiled=True)  17.6 us
    pmin x1, blocking collectives, nearest_local(): best = lax.pmin(local_min, 'cb')  11 us
    gather x1, local copies, waits for them, and re-layouts, local(): looked = jnp.take(codebook, code_one, axis=0)  9.38 us
    dot_general x2, matrix products, section_update(): lax.dot_general(onehot, data, (((0,), (0,)), ((), ())), preferred_element...  8.51 us
    dot_general x2, matrix products, nearest_local(): lax.dot_general(data, cents, (((1,), (1,)), ((), ())), preferred_element_...  6.18 us
  transfers between devices with their start and end apart: 3, of which 2 were waited for; matrix products, arithmetic and copies ran while one was open for 8% of the time, Pallas kernels for 0%

commit v1 on v0

--- a/solution.py
+++ b/solution.py
@@ -1,7 +1,343 @@
+import functools
+
 import jax
 import jax.numpy as jnp
 from jax import lax
+from jax.experimental import pallas as pl
+from jax.experimental.pallas import tpu as pltpu
 from jax.sharding import PartitionSpec as P
+
+F32 = jnp.float32
+BF16 = jnp.bfloat16
+CORES = 2
+
+
+def fused_kernel(
+    npts, ncb,
+    points, code_one, code_two, cent_one, cent_two,
+    new_one, new_two, total_out,
+    residual, codebook, sums, from_left, from_right, codes_all, mins, mins_in, tot, tot_in,
+    rs_send, rs_left, rs_right, ag_send, ag_left, ag_right,
+    x_send, x_recv, d_send, d_recv, code_send, code_recv, min_send, min_recv, tot_send, tot_recv,
+):
+    p = lax.axis_index("pts")
+    c = lax.axis_index("cb")
+    npoints, width = points.shape
+    rows = cent_one.shape[0]
+    share = rows // npts
+    ids = rows * ncb
+    nx = ncb // CORES
+    cx, cc = c // CORES, c % CORES
+    sibling = cx * CORES + (1 - cc)
+
+    def to_pts(src, dst, s, r, where):
+        return pltpu.make_async_remote_copy(
+            src_ref=src, dst_ref=dst, send_sem=s, recv_sem=r,
+            device_id={"pts": where}, device_id_type=pl.DeviceIdType.MESH,
+        )
+
+    def to_cb(src, dst, s, r, where):
+        return pltpu.make_async_remote_copy(
+            src_ref=src, dst_ref=dst, send_sem=s, recv_sem=r,
+            device_id={"cb": where}, device_id_type=pl.DeviceIdType.MESH,
+        )
+
+    barrier = pltpu.get_barrier_semaphore()
+    for d in range(1, npts):
+        pl.semaphore_signal(barrier, inc=1, device_id={"pts": (p + d) % npts},
+                            device_id_type=pl.DeviceIdType.MESH)
+    for d in range(1, ncb):
+        pl.semaphore_signal(barrier, inc=1, device_id={"cb": (c + d) % ncb},
+                            device_id_type=pl.DeviceIdType.MESH)
+
+    def partial_sums(data, code):
+        def one(t, carry):
+            label = c * rows + t * share + lax.broadcasted_iota(jnp.int32, (share, npoints), 0)
+            onehot = jnp.where(code[...] == label, 1.0, 0.0).astype(BF16)
+            sums[t] = jnp.dot(onehot, data[...], preferred_element_type=F32)
+            return carry
+
+        lax.fori_loop(0, npts, one, 0)
+
+    def send_right(k, t):
+        return to_pts(sums.at[t], from_left.at[k, t], rs_send.at[k, t], rs_left.at[k, t], p + 1)
+
+    def send_left(k, t):
+        return to_pts(sums.at[t], from_right.at[k, t], rs_send.at[k, t], rs_right.at[k, t], p - 1)
+
+    def reduce_first(k):
+        @pl.when(p == 0)
+        def _():
+            for s in range(npts - 1):
+                send_right(k, npts - 1 - s).start()
+
+        @pl.when(p == npts - 1)
+        def _():
+            for s in range(npts - 1):
+                send_left(k, s).start()
+
+    def reduce_rest(k):
+        inner = jnp.logical_and(p > 0, p < npts - 1)
+        for s in range(npts - 1):
+            t_right, t_left = npts - 1 - s, s
+
+            @pl.when(jnp.logical_and(inner, p < t_right))
+            def _():
+                send_right(k, t_right).wait_recv()
+                sums[t_right] += from_left[k, t_right]
+                send_right(k, t_right).start()
+
+            @pl.when(jnp.logical_and(inner, p > t_left))
+            def _():
+                send_left(k, t_left).wait_recv()
+                sums[t_left] += from_right[k, t_left]
+                send_left(k, t_left).start()
+
+    def reduce_last(k):
+        @pl.when(p > 0)
+        def _():
+            send_right(k, p).wait_recv()
+            sums[p] += from_left[k, p]
+
+        @pl.when(p < npts - 1)
+        def _():
+            send_left(k, p).wait_recv()
+            sums[p] += from_right[k, p]
+
+    def reduce_sent(k):
+        for t in range(npts):
+            @pl.when(p < t)
+            def _():
+                send_right(k, t).wait_send()
+
+            @pl.when(p > t)
+            def _():
+                send_left(k, t).wait_send()
+
+    def counts(k):
+        label = c * rows + p * share + lax.broadcasted_iota(jnp.int32, (share, npoints), 0)
+
+        def one(t, acc):
+            return acc + jnp.where(codes_all[k, t] == label, 1.0, 0.0)
+
+        acc = lax.fori_loop(0, npts, one, jnp.zeros((share, npoints), F32))
+        return jnp.sum(acc, axis=1, keepdims=True)
+
+    def finish(k, cents, count, out, at):
+        old = cents[pl.ds(pl.multiple_of(p * share, share), share), :].astype(F32)
+        out[pl.ds(at, share), :] = ((sums[p] + old) / (count + 1.0)).astype(BF16)
+
+    def nearest(k, data, cents):
+        step = npoints // 8
+        cent = cents[...]
+        csq = jnp.sum(jnp.square(cent.astype(F32)), axis=1, keepdims=True)
+        scaled = cent * (-2.0)
+
+        def one(i, acc):
+            at = pl.ds(pl.multiple_of(i * step, step), step)
+            block = data[at, :]
+            cross = lax.dot_general(scaled.astype(BF16), block, (((1,), (1,)), ((), ())),
+                                    preferred_element_type=F32)
+            mins[k, :, at] = jnp.min(cross + csq, axis=0, keepdims=True)
+            sq = jnp.square(block.astype(F32))
+            return acc + jnp.sum(sq.reshape(step // 8, 8, width), axis=0)
+
+        acc = lax.fori_loop(0, 8, one, jnp.zeros((8, width), F32))
+        return jnp.sum(acc, keepdims=True)
+
+    def row_block(col, t):
+        return pl.ds(pl.multiple_of(col * rows + t * share, share), share)
+
+    partial_sums(points, code_one)
+    pl.semaphore_wait(barrier, npts - 1 + ncb - 1)
+    reduce_first(0)
+    for k, code in enumerate((code_one, code_two)):
+        for d in range(1, npts):
+            to_pts(code, codes_all.at[k, p], code_send.at[k, d], code_recv.at[k, d],
+                   (p + d) % npts).start()
+        codes_all[k, p] = code[...]
+    sq_one = nearest(0, points, cent_one)
+    for k, code in enumerate((code_one, code_two)):
+        for d in range(1, npts):
+            to_pts(code, codes_all.at[k, (p + npts - d) % npts], code_send.at[k, d],
+                   code_recv.at[k, d], (p + d) % npts).wait()
+    count_one = counts(0)
+    reduce_rest(0)
+    count_two = counts(1)
+    reduce_last(0)
+    reduce_sent(0)
+    finish(0, cent_one, count_one, codebook, pl.multiple_of(c * rows + p * share, share))
+
+    def ag_right_copy(t):
+        block = codebook.at[row_block(c, t), :]
+        return to_pts(block, block, ag_send.at[0, t], ag_left.at[t], p + 1)
+
+    def ag_left_copy(t):
+        block = codebook.at[row_block(c, t), :]
+        return to_pts(block, block, ag_send.at[1, t], ag_right.at[t], p - 1)
+
+    def x_copy(o, t, col):
+        block = codebook.at[row_block(col, t), :]
+        return to_cb(block, block, x_send.at[o, t], x_recv.at[o, t], ((cx + o) % nx) * CORES + cc)
+
+    def d_copy(o, t, col):
+        block = codebook.at[row_block(col, t), :]
+        return to_cb(block, block, d_send.at[o, t], d_recv.at[o, t], sibling)
+
+    def spread(t):
+        for o in range(1, nx):
+            x_copy(o, t, c).start()
+        d_copy(0, t, c).start()
+
+    def gather_own(do_spread, right_copy, left_copy):
+        for s in range(npts):
+            for way in ((0,) if s == 0 else (0, 1)):
+                t = p - s if way == 0 else p + s
+
+                @pl.when(jnp.logical_and(t >= 0, t < npts))
+                def _():
+                    if s > 0 and way == 0:
+                        right_copy(t).wait_recv()
+                    if s > 0 and way == 1:
+                        left_copy(t).wait_recv()
+                    if way == 0:
+                        @pl.when(p < npts - 1)
+                        def _():
+                            right_copy(t).start()
+                    if way == 1 or s == 0:
+                        @pl.when(p > 0)
+                        def _():
+                            left_copy(t).start()
+                    if do_spread:
+                        spread(t)
+
+    def gather_own_sent(right_copy, left_copy):
+        for t in range(npts):
+            @pl.when(jnp.logical_and(t <= p, p < npts - 1))
+            def _():
+                right_copy(t).wait_send()
+
+            @pl.when(jnp.logical_and(t >= p, p > 0))
+            def _():
+                left_copy(t).wait_send()
+
+    gather_own(True, ag_right_copy, ag_left_copy)
+    for s in range(npts):
+        for way in ((0,) if s == 0 else (0, 1)):
+            t = p - s if way == 0 else p + s
+
+            @pl.when(jnp.logical_and(t >= 0, t < npts))
+            def _():
+                for o in range(1, nx):
+                    src = ((cx + nx - o) % nx) * CORES + cc
+                    x_copy(o, t, src).wait_recv()
+                    d_copy(o, t, src).start()
+    for t in range(npts):
+        for o in range(nx):
+            d_copy(o, t, ((cx + nx - o) % nx) * CORES + 1 - cc).wait_recv()
+    for t in range(npts):
+        for o in range(nx):
+            d_copy(o, t, ((cx + nx - o) % nx) * CORES + cc).wait_send()
+            if o > 0:
+                x_copy(o, t, c).wait_send()
+    gather_own_sent(ag_right_copy, ag_left_copy)
+    new_one[...] = codebook[pl.ds(pl.multiple_of(c * rows, rows), rows), :]
+
+    tile = 128
+    group = 4
+
+    def look(i, carry):
+        blocks = []
+        for j in range(group):
+            at = pl.ds(pl.multiple_of((i * group + j) * tile, tile), tile)
+            blocks.append(jnp.broadcast_to(code_one[:, at], (tile, tile)).T)
+        column = jnp.concatenate(blocks, axis=0)
+        wide = jnp.concatenate([column] * (ids // tile), axis=1)
+        label = lax.broadcasted_iota(jnp.int32, (group * tile, ids), 1)
+        onehot = jnp.where(wide == label, 1.0, 0.0).astype(BF16)
+        looked = jnp.dot(onehot, codebook[...], preferred_element_type=F32)
+        at = pl.ds(pl.multiple_of(i * group * tile, group * tile), group * tile)
+        residual[at, :] = (points[at, :].astype(F32) - looked).astype(BF16)
+        return carry
+
+    lax.fori_loop(0, npoints // (group * tile), look, 0)
+
+    partial_sums(residual, code_two)
+    reduce_first(1)
+    sq_two = nearest(1, residual, cent_two)
+    for d in range(1, ncb):
+        to_cb(mins, mins_in.at[d], min_send.at[d], min_recv.at[d], (c + d) % ncb).start()
+    reduce_rest(1)
+    for d in range(1, ncb):
+        to_cb(mins, mins_in.at[d], min_send.at[d], min_recv.at[d], (c + d) % ncb).wait()
+    best = mins[...]
+    for d in range(1, ncb):
+        best = jnp.minimum(best, mins_in[d])
+    for k, sq in enumerate((sq_one, sq_two)):
+        tot[k] = jnp.broadcast_to(jnp.sum(best[k], keepdims=True) + sq, tot.shape[1:])
+    for d in range(1, npts):
+        to_pts(tot, tot_in.at[d], tot_send.at[d], tot_recv.at[d], (p + d) % npts).start()
+    reduce_last(1)
+    reduce_sent(1)
+    finish(1, cent_two, count_two, new_two, pl.multiple_of(p * share, share))
+
+    def two_right_copy(t):
+        block = new_two.at[pl.ds(pl.multiple_of(t * share, share), share), :]
+        return to_pts(block, block, ag_send.at[2, t], ag_left.at[npts + t], p + 1)
+
+    def two_left_copy(t):
+        block = new_two.at[pl.ds(pl.multiple_of(t * share, share), share), :]
+        return to_pts(block, block, ag_send.at[3, t], ag_right.at[npts + t], p - 1)
+
+    gather_own(False, two_right_copy, two_left_copy)
+    for d in range(1, npts):
+        to_pts(tot, tot_in.at[d], tot_send.at[d], tot_recv.at[d], (p + d) % npts).wait()
+    total = tot[...]
+    for d in range(1, npts):
+        total = total + tot_in[d]
+    total_out[...] = total / F32(npoints * npts * width)
+    gather_own_sent(two_right_copy, two_left_copy)
+
+
+def fused(points, code_one, code_two, cent_one, cent_two):
+    npts = lax.axis_size("pts")
+    ncb = lax.axis_size("cb")
+    npoints, width = points.shape
+    rows = cent_one.shape[0]
+    share = rows // npts
+    nx = ncb // CORES
+    vmem = pl.BlockSpec(memory_space=pltpu.VMEM)
+    dma = pltpu.SemaphoreType.DMA
+    new_one, new_two, total = pl.pallas_call(
+        functools.partial(fused_kernel, npts, ncb),
+        out_shape=(
+            jax.ShapeDtypeStruct(cent_one.shape, BF16),
+            jax.ShapeDtypeStruct(cent_two.shape, BF16),
+            jax.ShapeDtypeStruct((2, 1, 128), F32),
+        ),
+        in_specs=[vmem] * 5,
+        out_specs=(vmem,) * 3,
+        scratch_shapes=[
+            pltpu.VMEM(points.shape, BF16),
+            pltpu.VMEM((rows * ncb, width), BF16),
+            pltpu.VMEM((npts, share, width), F32),
+            pltpu.VMEM((2, npts, share, width), F32),
+            pltpu.VMEM((2, npts, share, width), F32),
+            pltpu.VMEM((2, npts, 1, npoints), jnp.int32),
+            pltpu.VMEM((2, 1, npoints), F32),
+            pltpu.VMEM((ncb, 2, 1, npoints), F32),
+            pltpu.VMEM((2, 1, 128), F32),
+            pltpu.VMEM((npts, 2, 1, 128), F32),
+            dma((2, npts)), dma((2, npts)), dma((2, npts)),
+            dma((4, npts)), dma((2 * npts,)), dma((2 * npts,)),
+            dma((nx, npts)), dma((nx, npts)), dma((nx, npts)), dma((nx, npts)),
+            dma((2, npts)), dma((2, npts)), dma((ncb,)), dma((ncb,)), dma((npts,)), dma((npts,)),
+        ],
+        compiler_params=pltpu.CompilerParams(
+            collective_id=0, has_side_effects=True, vmem_limit_bytes=60 * 1024 * 1024
+        ),
+    )(points, code_one.reshape(1, npoints), code_two.reshape(1, npoints), cent_one, cent_two)
+    return new_one, new_two, total[:, 0, 0]
 
 
 def nearest_local(data, cents):
@@ -66,9 +402,16 @@
     return (new_one, new_two, distortion)
 
 
+def choose(points, code_one, code_two, cent_one, cent_two):
+    rows, npts, ncb = cent_one.shape[0], lax.axis_size("pts"), lax.axis_size("cb")
+    fits = rows % (16 * npts) == 0 and ncb % CORES == 0 and points.shape[0] % 1024 == 0
+    form = fused if fits else local
+    return form(points, code_one, code_two, cent_one, cent_two)
+
+
 def solution(mesh):
     return jax.shard_map(
-        local,
+        choose,
         mesh=mesh,
         in_specs=(
             P(("groups", "pts"), None),

time: 181 us -> 161 us (0.89)
  Pallas kernels: 0 us -> 155 us
  waiting for transfers between devices: 67.3 us -> 0 us
  blocking collectives: 53.6 us -> 0 us
  matrix products: 14.7 us -> 0 us
  other arithmetic: 14.5 us -> 0 us
  between operations: 14.6 us -> 0.64 us
  local copies, waits for them, and re-layouts: 15.6 us -> 5.4 us
    pallas_call x0 -> x1, Pallas kernels: none -> 155 us  [fused(): pl.pallas_call(functools.partial(fused_kernel, npts, ncb), out_shape=(jax...]
    all_gather x1 -> x0, waiting for transfers between devices: 45.4 us -> none  [local(): gathered = lax.all_gather(updated_one, ('pts', 'cb'), axis=0, tiled=True)]
    unnamed x2 -> x0, blocking collectives: 25 us -> none
    reduce_scatter x2 -> x0, waiting for transfers between devices: 21.9 us -> none  [section_update(): lax.psum_scatter(sums, 'pts', scatter_dimension=0, tiled=True)]
    all_gather x1 -> x0, blocking collectives: 17.6 us -> none  [local(): new_two = lax.all_gather(updated_two, 'pts', axis=0, tiled=True)]
    dot_general x4 -> x0, matrix products: 14.7 us -> none  [the longest x2 8.51 us: section_update(): lax.dot_general(onehot, data, (((0,), (0,)), ((), ())), preferred_element...]
    pmin x1 -> x0, blocking collectives: 11 us -> none  [nearest_local(): best = lax.pmin(local_min, 'cb')]
    reduce_sum x6 -> x0, other arithmetic: 9.5 us -> none  [the longest x1 4.34 us: nearest_local(): sq = jnp.sum(jnp.square(data.astype(jnp.float32)), axis=1)]
  transfers between devices with their start and end apart: 3 -> 0, of which waited for: 2 -> 0; matrix products, arithmetic and copies ran while one was open for 8% -> 0% of each run, Pallas kernels for 0% -> 0%
where the time goes in v1:
time: 161 us
  Pallas kernels  155 us (96%)
  local copies, waits for them, and re-layouts  5.4 us (3%)
    pallas_call x1, Pallas kernels, fused(): pl.pallas_call(functools.partial(fused_kernel, npts, ncb), out_shape=(jax...  155 us
    unnamed x2, local copies, waits for them, and re-layouts  4.12 us

profile of v1, /device:TPU:0, one launch (start us, length us, event | category | flops | bytes accessed | tf_op | source)
XLA Modules:
  0.0 160.7 jit_solution(4379489300958219123)
XLA Ops:
  0.6 154.7 %shard_map.76 = (bf16[512,768]{1,0:T(8,128)(2,1)}, bf16[512,768]{1,0:T(8,128)(2,1)}, f32[2,1,128]{2,1,0:T(1,128)}) custom-call(bf16[2048,768]{1,0:T(8,128)(2,1)} %points.1, s32[1,2048]{1,0:T(1,128)} %bitcast.2, s32[1,2048]{1,0:T(1,128)} %bitcast.3, bf16[512,768]{1,0:T(8,128)(2,1)} %cent_one.1, bf16[512,768]{1,0:T(8,128)(2,1)} %cent_two.1), custom_call_target="tpu_custom_call" | custom-call | tf_op jit(solution)/shard_map/pallas_call | solution.py:311
  155.3 1.3 slice_reduce_fusion
  156.6 2.1 %copy.10 = bf16[512,768]{1,0:T(8,128)(2,1)} copy(bf16[512,768]{1,0:T(8,128)(2,1)} %get-tuple-element.12) | data formatting | bytes 1572864
  158.6 2.1 %copy.11 = bf16[512,768]{1,0:T(8,128)(2,1)} copy(bf16[512,768]{1,0:T(8,128)(2,1)} %get-tuple-element.13) | data formatting | bytes 1572864

commit v2 on v0

--- a/solution.py
+++ b/solution.py
@@ -1,7 +1,335 @@
+import functools
+
 import jax
 import jax.numpy as jnp
 from jax import lax
+from jax.experimental import pallas as pl
+from jax.experimental.pallas import tpu as pltpu
 from jax.sharding import PartitionSpec as P
+
+F32 = jnp.float32
+BF16 = jnp.bfloat16
+CORES = 2
+PARTS = 8
+LAG = 2
+WINDOW = 2
+
+
+def fused_kernel(
+    npts, ncb, parts, lag, window,
+    points, code_one, code_two, cent_one, cent_two,
+    new_one, new_two, total_out,
+    residual, codebook, sums, from_left, from_right, codes_all, mins, mins_in, tot, tot_in,
+    scaled, csq, squares,
+    rs_send, rs_recv, ag_send, ag_recv,
+    x_send, x_recv, d_send, d_recv, code_send, code_recv, min_send, min_recv, tot_send, tot_recv,
+):
+    p = lax.axis_index("pts")
+    c = lax.axis_index("cb")
+    last = npts - 1
+    npoints, width = points.shape
+    rows = cent_one.shape[0]
+    size = rows // (2 * parts)
+    ids = rows * ncb
+    nx = ncb // CORES
+    cx, cc = c // CORES, c % CORES
+    sibling = cx * CORES + (1 - cc)
+
+    def to(axis, src, dst, s, r, where):
+        return pltpu.make_async_remote_copy(
+            src_ref=src, dst_ref=dst, send_sem=s, recv_sem=r,
+            device_id={axis: where}, device_id_type=pl.DeviceIdType.MESH,
+        )
+
+    barrier = pltpu.get_barrier_semaphore()
+    for d in range(1, npts):
+        pl.semaphore_signal(barrier, inc=1, device_id={"pts": (p + d) % npts},
+                            device_id_type=pl.DeviceIdType.MESH)
+    for d in range(1, ncb):
+        pl.semaphore_signal(barrier, inc=1, device_id={"cb": (c + d) % ncb},
+                            device_id_type=pl.DeviceIdType.MESH)
+
+    span = rows // npts
+
+    def partial_sums(data, code):
+        def one(t, carry):
+            label = c * rows + t * span + lax.broadcasted_iota(jnp.int32, (span, npoints), 0)
+            onehot = jnp.where(code[...] == label, 1.0, 0.0).astype(BF16)
+            at = pl.ds(pl.multiple_of(t * span, span), span)
+            sums[at, :] = jnp.dot(onehot, data[...], preferred_element_type=F32)
+            return carry
+
+        lax.fori_loop(0, npts, one, 0)
+
+    def code_copy(k, d, slot):
+        code = (code_one, code_two)[k]
+        return to("pts", code, codes_all.at[k, slot], code_send.at[k, d], code_recv.at[k, d],
+                  (p + d) % npts)
+
+    def part(g):
+        return pl.ds(pl.multiple_of(g * size, size), size)
+
+    def count(k, g):
+        label = c * rows + g * size + lax.broadcasted_iota(jnp.int32, (size, npoints), 0)
+        acc = jnp.zeros((size, npoints), F32)
+        for t in range(npts):
+            acc = acc + jnp.where(codes_all[k, t] == label, 1.0, 0.0)
+        return jnp.sum(acc, axis=1, keepdims=True)
+
+    pieces = 8
+    step = npoints // pieces
+
+    def near_start(cents):
+        cent = cents[...]
+        csq[...] = jnp.sum(jnp.square(cent.astype(F32)), axis=1, keepdims=True)
+        scaled[...] = (cent * (-2.0)).astype(BF16)
+        squares[...] = jnp.zeros(squares.shape, F32)
+
+    def near_piece(k, data, i):
+        at = pl.ds(pl.multiple_of(i * step, step), step)
+        block = data[at, :]
+        cross = lax.dot_general(scaled[...], block, (((1,), (1,)), ((), ())),
+                                preferred_element_type=F32)
+        mins[k, :, at] = jnp.min(cross + csq[...], axis=0, keepdims=True)
+        sq = jnp.square(block.astype(F32))
+        squares[...] += jnp.sum(sq.reshape(step // 8, 8, width), axis=0)
+
+    def exchange(k, data, cents, table, base, share_out):
+        def row(g):
+            return table.at[pl.ds(pl.multiple_of(base + g * size, size), size), :]
+
+        def rs(way, j):
+            g = j + (parts if way == 1 else 0)
+            land = from_left if way == 1 else from_right
+            return to("pts", sums.at[part(g), :], land.at[k, j], rs_send.at[k, way, j],
+                      rs_recv.at[k, way, j], p + 1 if way == 1 else p - 1)
+
+        def ag(way, j):
+            g = j + (parts if way == 1 else 0)
+            return to("pts", row(g), row(g), ag_send.at[k, way, j], ag_recv.at[k, way, j],
+                      p - 1 if way == 1 else p + 1)
+
+        def block(col, g):
+            at = pl.multiple_of(col * rows + g * size, size)
+            return codebook.at[pl.ds(at, size), :]
+
+        def x_copy(o, g):
+            return to("cb", block(c, g), block(c, g), x_send.at[o, g], x_recv.at[o, g],
+                      ((cx + o) % nx) * CORES + cc)
+
+        def d_copy(o, g):
+            ref = block(((cx + nx - o) % nx) * CORES + cc, g)
+            return to("cb", ref, ref, d_send.at[o, g], d_recv.at[o, g], sibling)
+
+        def spread(g):
+            if share_out:
+                for o in range(1, nx):
+                    x_copy(o, g).start()
+                d_copy(0, g).start()
+
+        def run(i, carry):
+            for way in (1, 0):
+                first, end = (0, last) if way == 1 else (last, 0)
+                shift = parts if way == 1 else 0
+                near_end = p if way == 1 else last - p
+                j = i - lag * near_end
+
+                @pl.when(jnp.logical_and(j >= 0, j < parts))
+                def _():
+                    @pl.when(p != first)
+                    def _():
+                        rs(way, j).wait_recv()
+                        land = from_left if way == 1 else from_right
+                        sums[part(j + shift), :] += land[k, j]
+
+                    @pl.when(p != end)
+                    def _():
+                        @pl.when(j >= window)
+                        def _():
+                            rs(way, j - window).wait_send()
+
+                        rs(way, j).start()
+
+                    @pl.when(p == end)
+                    def _():
+                        g = j + shift
+                        old = cents[part(g), :].astype(F32)
+                        row(g)[...] = (
+                            (sums[part(g), :] + old) / (count(k, g) + 1.0)
+                        ).astype(BF16)
+                        ag(way, j).start()
+                        spread(g)
+
+                back = i - lag * (2 * last) + lag * near_end
+
+                @pl.when(jnp.logical_and(p != end, jnp.logical_and(back >= 0, back < parts)))
+                def _():
+                    ag(way, back).wait_recv()
+
+                    @pl.when(p != first)
+                    def _():
+                        ag(way, back).start()
+
+                    spread(back + shift)
+
+                if share_out:
+                    over = back - lag
+
+                    @pl.when(jnp.logical_and(over >= 0, over < parts))
+                    def _():
+                        for o in range(1, nx):
+                            x_copy(o, over + shift).wait_recv()
+                            d_copy(o, over + shift).start()
+
+            @pl.when(i < pieces)
+            def _():
+                near_piece(k, data, i)
+
+            if k == 0:
+                @pl.when(i == lag)
+                def _():
+                    for kk in range(2):
+                        for d in range(1, npts):
+                            code_copy(kk, d, (p + npts - d) % npts).wait()
+            else:
+                @pl.when(i == pieces)
+                def _():
+                    for d in range(1, ncb):
+                        min_copy(d).start()
+
+                @pl.when(i == pieces + 2 * lag)
+                def _():
+                    totals()
+
+            return carry
+
+        steps = parts + 2 * lag * last + (lag if share_out else 0)
+        lax.fori_loop(0, max(steps, pieces + 2 * lag + 1), run, 0)
+
+        def drain(j, carry):
+            for way in (1, 0):
+                first, end = (0, last) if way == 1 else (last, 0)
+                shift = parts if way == 1 else 0
+
+                @pl.when(jnp.logical_and(p != end, j >= parts - window))
+                def _():
+                    rs(way, j).wait_send()
+
+                @pl.when(p != first)
+                def _():
+                    ag(way, j).wait_send()
+
+                if share_out:
+                    for o in range(nx):
+                        d_copy(o, j + shift).wait()
+                        if o > 0:
+                            x_copy(o, j + shift).wait_send()
+            return carry
+
+        lax.fori_loop(0, parts, drain, 0)
+
+    def min_copy(d):
+        return to("cb", mins, mins_in.at[d], min_send.at[d], min_recv.at[d], (c + d) % ncb)
+
+    def tot_copy(d):
+        return to("pts", tot, tot_in.at[d], tot_send.at[d], tot_recv.at[d], (p + d) % npts)
+
+    def totals():
+        for d in range(1, ncb):
+            min_copy(d).wait()
+        best = mins[...]
+        for d in range(1, ncb):
+            best = jnp.minimum(best, mins_in[d])
+        squares_two = jnp.sum(squares[...], keepdims=True)
+        for k in range(2):
+            sq = squares_two if k == 1 else tot[0, :, :1]
+            tot[k] = jnp.broadcast_to(jnp.sum(best[k], keepdims=True) + sq, tot.shape[1:])
+        for d in range(1, npts):
+            tot_copy(d).start()
+
+    partial_sums(points, code_one)
+    near_start(cent_one)
+    pl.semaphore_wait(barrier, npts - 1 + ncb - 1)
+    for k, code in enumerate((code_one, code_two)):
+        for d in range(1, npts):
+            code_copy(k, d, p).start()
+        codes_all[k, p] = code[...]
+    exchange(0, points, cent_one, codebook, c * rows, True)
+    tot[0] = jnp.broadcast_to(jnp.sum(squares[...], keepdims=True), tot.shape[1:])
+
+    tile = 128
+    group = 4
+
+    def look(i, carry):
+        blocks = []
+        for j in range(group):
+            at = pl.ds(pl.multiple_of((i * group + j) * tile, tile), tile)
+            blocks.append(jnp.broadcast_to(code_one[:, at], (tile, tile)).T)
+        column = jnp.concatenate(blocks, axis=0)
+        wide = jnp.concatenate([column] * (ids // tile), axis=1)
+        label = lax.broadcasted_iota(jnp.int32, (group * tile, ids), 1)
+        onehot = jnp.where(wide == label, 1.0, 0.0).astype(BF16)
+        looked = jnp.dot(onehot, codebook[...], preferred_element_type=F32)
+        at = pl.ds(pl.multiple_of(i * group * tile, group * tile), group * tile)
+        residual[at, :] = (points[at, :].astype(F32) - looked).astype(BF16)
+        return carry
+
+    lax.fori_loop(0, npoints // (group * tile), look, 0)
+    partial_sums(residual, code_two)
+    near_start(cent_two)
+    exchange(1, residual, cent_two, new_two, 0, False)
+    new_one[...] = codebook[pl.ds(pl.multiple_of(c * rows, rows), rows), :]
+    for d in range(1, npts):
+        tot_copy(d).wait()
+    total = tot[...]
+    for d in range(1, npts):
+        total = total + tot_in[d]
+    total_out[...] = total / F32(npoints * npts * width)
+
+
+def fused(points, code_one, code_two, cent_one, cent_two):
+    npts = lax.axis_size("pts")
+    ncb = lax.axis_size("cb")
+    npoints, width = points.shape
+    rows = cent_one.shape[0]
+    nx = ncb // CORES
+    parts = PARTS
+    size = rows // (2 * parts)
+    vmem = pl.BlockSpec(memory_space=pltpu.VMEM)
+    dma = pltpu.SemaphoreType.DMA
+    new_one, new_two, total = pl.pallas_call(
+        functools.partial(fused_kernel, npts, ncb, parts, LAG, WINDOW),
+        out_shape=(
+            jax.ShapeDtypeStruct(cent_one.shape, BF16),
+            jax.ShapeDtypeStruct(cent_two.shape, BF16),
+            jax.ShapeDtypeStruct((2, 1, 128), F32),
+        ),
+        in_specs=[vmem] * 5,
+        out_specs=(vmem,) * 3,
+        scratch_shapes=[
+            pltpu.VMEM(points.shape, BF16),
+            pltpu.VMEM((rows * ncb, width), BF16),
+            pltpu.VMEM((rows, width), F32),
+            pltpu.VMEM((2, parts, size, width), F32),
+            pltpu.VMEM((2, parts, size, width), F32),
+            pltpu.VMEM((2, npts, 1, npoints), jnp.int32),
+            pltpu.VMEM((2, 1, npoints), F32),
+            pltpu.VMEM((ncb, 2, 1, npoints), F32),
+            pltpu.VMEM((2, 1, 128), F32),
+            pltpu.VMEM((npts, 2, 1, 128), F32),
+            pltpu.VMEM((rows, width), BF16),
+            pltpu.VMEM((rows, 1), F32),
+            pltpu.VMEM((8, width), F32),
+            dma((2, 2, parts)), dma((2, 2, parts)), dma((2, 2, parts)), dma((2, 2, parts)),
+            dma((nx, 2 * parts)), dma((nx, 2 * parts)), dma((nx, 2 * parts)),
+            dma((nx, 2 * parts)),
+            dma((2, npts)), dma((2, npts)), dma((ncb,)), dma((ncb,)), dma((npts,)), dma((npts,)),
+        ],
+        compiler_params=pltpu.CompilerParams(
+            collective_id=0, has_side_effects=True, vmem_limit_bytes=60 * 1024 * 1024
+        ),
+    )(points, code_one.reshape(1, npoints), code_two.reshape(1, npoints), cent_one, cent_two)
+    return new_one, new_two, total[:, 0, 0]
 
 
 def nearest_local(data, cents):
@@ -66,9 +394,22 @@
     return (new_one, new_two, distortion)
 
 
+def choose(points, code_one, code_two, cent_one, cent_two):
+    rows, npts, ncb = cent_one.shape[0], lax.axis_size("pts"), lax.axis_size("cb")
+    fits = (
+        1 < npts <= 8
+        and rows % (32 * PARTS) == 0
+        and rows % (16 * npts) == 0
+        and ncb % CORES == 0
+        and points.shape[0] % 1024 == 0
+    )
+    form = fused if fits else local
+    return form(points, code_one, code_two, cent_one, cent_two)
+
+
 def solution(mesh):
     return jax.shard_map(
-        local,
+        choose,
         mesh=mesh,
         in_specs=(
             P(("groups", "pts"), None),

time: 181 us -> 113 us (0.62)
  Pallas kernels: 0 us -> 107 us
  waiting for transfers between devices: 67.3 us -> 0 us
  blocking collectives: 53.6 us -> 0 us
  matrix products: 14.7 us -> 0 us
  other arithmetic: 14.5 us -> 0 us
  between operations: 14.6 us -> 0.64 us
  local copies, waits for them, and re-layouts: 15.6 us -> 5.4 us
    pallas_call x0 -> x1, Pallas kernels: none -> 107 us  [fused(): pl.pallas_call(functools.partial(fused_kernel, npts, ncb, parts, LAG, WIN...]
    all_gather x1 -> x0, waiting for transfers between devices: 45.4 us -> none  [local(): gathered = lax.all_gather(updated_one, ('pts', 'cb'), axis=0, tiled=True)]
    unnamed x2 -> x0, blocking collectives: 25 us -> none
    reduce_scatter x2 -> x0, waiting for transfers between devices: 21.9 us -> none  [section_update(): lax.psum_scatter(sums, 'pts', scatter_dimension=0, tiled=True)]
    all_gather x1 -> x0, blocking collectives: 17.6 us -> none  [local(): new_two = lax.all_gather(updated_two, 'pts', axis=0, tiled=True)]
    dot_general x4 -> x0, matrix products: 14.7 us -> none  [the longest x2 8.51 us: section_update(): lax.dot_general(onehot, data, (((0,), (0,)), ((), ())), preferred_element...]
    pmin x1 -> x0, blocking collectives: 11 us -> none  [nearest_local(): best = lax.pmin(local_min, 'cb')]
    reduce_sum x6 -> x0, other arithmetic: 9.5 us -> none  [the longest x1 4.34 us: nearest_local(): sq = jnp.sum(jnp.square(data.astype(jnp.float32)), axis=1)]
  transfers between devices with their start and end apart: 3 -> 0, of which waited for: 2 -> 0; matrix products, arithmetic and copies ran while one was open for 8% -> 0% of each run, Pallas kernels for 0% -> 0%
where the time goes in v2:
time: 113 us
  Pallas kernels  107 us (95%)
  local copies, waits for them, and re-layouts  5.4 us (5%)
    pallas_call x1, Pallas kernels, fused(): pl.pallas_call(functools.partial(fused_kernel, npts, ncb, parts, LAG, WIN...  107 us
    unnamed x2, local copies, waits for them, and re-layouts  4.12 us

profile of v2, /device:TPU:0, one launch (start us, length us, event | category | flops | bytes accessed | tf_op | source)
XLA Modules:
  0.0 112.7 jit_solution(9097321575968252791)
XLA Ops:
  0.6 106.7 %shard_map.76 = (bf16[512,768]{1,0:T(8,128)(2,1)}, bf16[512,768]{1,0:T(8,128)(2,1)}, f32[2,1,128]{2,1,0:T(1,128)}) custom-call(bf16[2048,768]{1,0:T(8,128)(2,1)} %points.1, s32[1,2048]{1,0:T(1,128)} %bitcast.2, s32[1,2048]{1,0:T(1,128)} %bitcast.3, bf16[512,768]{1,0:T(8,128)(2,1)} %cent_one.1, bf16[512,768]{1,0:T(8,128)(2,1)} %cent_two.1), custom_call_target="tpu_custom_call" | custom-call | tf_op jit(solution)/shard_map/pallas_call | solution.py:300
  107.3 1.3 %slice_reduce_fusion = f32[2]{0:T(128)} fusion(f32[2,1,128]{2,1,0:T(1,128)} %get-tuple-element.8), kind=kLoop, calls=%fused_computation | loop fusion | bytes 16 | tf_op jit(solution)/shard_map/slice | solution.py:332
  108.6 2.1 %copy.10 = bf16[512,768]{1,0:T(8,128)(2,1)} copy(bf16[512,768]{1,0:T(8,128)(2,1)} %get-tuple-element.12) | data formatting | bytes 1572864
  110.6 2.1 %copy.11 = bf16[512,768]{1,0:T(8,128)(2,1)} copy(bf16[512,768]{1,0:T(8,128)(2,1)} %get-tuple-element.13) | data formatting | bytes 1572864

commit v3 on v2

--- a/solution.py
+++ b/solution.py
@@ -11,7 +11,7 @@
 BF16 = jnp.bfloat16
 CORES = 2
 PARTS = 8
-LAG = 2
+LAG = 3
 WINDOW = 2
 
 

time: 113 us -> 111 us (0.982)
  Pallas kernels: 107 us -> 105 us
    pallas_call x1, Pallas kernels: 107 us -> 105 us  [fused(): pl.pallas_call(functools.partial(fused_kernel, npts, ncb, parts, LAG, WIN...]
where the time goes in v3:
time: 111 us
  Pallas kernels  105 us (95%)
  local copies, waits for them, and re-layouts  5.4 us (5%)
    pallas_call x1, Pallas kernels, fused(): pl.pallas_call(functools.partial(fused_kernel, npts, ncb, parts, LAG, WIN...  105 us
    unnamed x2, local copies, waits for them, and re-layouts  4.12 us

profile of v3, /device:TPU:0, one launch (start us, length us, event | category | flops | bytes accessed | tf_op | source)
XLA Modules:
  0.0 111.2 jit_solution(5744142002388637611)
XLA Ops:
  0.6 105.2 %shard_map.76 = (bf16[512,768]{1,0:T(8,128)(2,1)}, bf16[512,768]{1,0:T(8,128)(2,1)}, f32[2,1,128]{2,1,0:T(1,128)}) custom-call(bf16[2048,768]{1,0:T(8,128)(2,1)} %points.1, s32[1,2048]{1,0:T(1,128)} %bitcast.2, s32[1,2048]{1,0:T(1,128)} %bitcast.3, bf16[512,768]{1,0:T(8,128)(2,1)} %cent_one.1, bf16[512,768]{1,0:T(8,128)(2,1)} %cent_two.1), custom_call_target="tpu_custom_call" | custom-call | tf_op jit(solution)/shard_map/pallas_call | solution.py:300
  105.8 1.3 %slice_reduce_fusion = f32[2]{0:T(128)} fusion(f32[2,1,128]{2,1,0:T(1,128)} %get-tuple-element.8), kind=kLoop, calls=%fused_computation | loop fusion | bytes 16 | tf_op jit(solution)/shard_map/slice | solution.py:332
  107.1 2.1 %copy.10 = bf16[512,768]{1,0:T(8,128)(2,1)} copy(bf16[512,768]{1,0:T(8,128)(2,1)} %get-tuple-element.12) | data formatting | bytes 1572864
  109.2 2.1 %copy.11 = bf16[512,768]{1,0:T(8,128)(2,1)} copy(bf16[512,768]{1,0:T(8,128)(2,1)} %get-tuple-element.13) | data formatting | bytes 1572864
